TPU v7x, 32 devices: a whole 2x2x4 slice. The times are simulated.
32 devices in a mesh: seq: 8 (over y, x, core), vocab: 4 (over z).
Axes of the slice: x: 2, y: 2, z: 4, core: 2. Of those that a mesh axis runs over, the one named last changes fastest.
Arguments:
- hidden: bfloat16 [960, 4096], P('seq'), may hold values from -32 to 32
- head_weight: bfloat16 [4096, 98304], P(None, ('seq', 'vocab')), may hold values from -0.84375 to 0.84375
- labels: int32 [960], P('seq'), may hold values from 0 to 98303
- lengths: int32 [8], replicated, may hold values from 1 to 120, 480 in all
- pair_map: int32 [8], replicated, may hold values from 0 to 7, each once
- ref_margin: float32 [4], replicated, may hold values from -240 to 240
Outputs:
- seq_logps: float32 [8], replicated
- pair_loss: float32 [4], replicated
- z_loss: float32 [], replicated
Inputs may be any that keep to these rules, and one draw needn't show every extreme that they name: The lengths sum to 480 and the longest is exactly 120. Each response appears once; pair p compares response pair_map[2p], chosen, with response pair_map[2p+1], rejected.
All inputs are finite; a program needn't handle non-finite values.
Results may differ from a plain program's by a relative error of at most 0.0003.
Values may be sent and summed in bfloat16 or wider, within the bound.
No kernel may reach another device: no remote copies, remote signals or barrier semaphores. Data moves between devices by JAX's collectives and lax.ppermute only.
A program may use at most 192 MiB of HBM per device.

v0:
```python
import jax
import jax.numpy as jnp
from jax import lax
from jax.sharding import PartitionSpec as P

pref_beta = 0.05
zloss_weight = 0.0001


def per_device(hidden, head_weight, labels, lengths, pair_map, ref_margin):
    vocab_devices = lax.axis_size("vocab")
    shard_rows = hidden.shape[0]
    columns = head_weight.shape[1]
    seq_total = lengths.shape[0]
    col_first = (lax.axis_index("seq") * vocab_devices + lax.axis_index("vocab")) * columns
    col_ids = col_first + jnp.arange(columns, dtype=jnp.int32)
    seq_ids = jnp.arange(seq_total, dtype=jnp.int32)
    logits = jnp.dot(
        lax.all_gather(hidden, "seq", axis=0, tiled=True),
        head_weight,
        preferred_element_type=jnp.float32,
    )
    local_max = jnp.max(logits, axis=1)
    local_sum = jnp.sum(jnp.exp(logits - local_max[:, None]), axis=1)
    picked = jnp.sum(
        jnp.where(
            lax.all_gather(labels, "seq", axis=0, tiled=True)[:, None] == col_ids[None, :],
            logits,
            0.0,
        ),
        axis=1,
    )
    fresh = (local_max, local_sum, picked)
    local_max, local_sum, picked = tuple((fresh_part for fresh_part in fresh))
    top_score = lax.pmax(local_max, ("seq", "vocab"))
    exp_total, label_logit = lax.psum(
        (local_sum * jnp.exp(local_max - top_score), picked), ("seq", "vocab")
    )
    log_norm = (top_score + jnp.log(exp_total)).reshape(seq_total, shard_rows)
    label_logit = label_logit.reshape(seq_total, shard_rows)
    live_mask = jnp.arange(shard_rows, dtype=jnp.int32)[None, :] < lengths[:, None]
    seq_logps = jnp.sum(jnp.where(live_mask, label_logit - log_norm, 0.0), axis=1)
    select = (pair_map[:, None] == seq_ids[None, :]).astype(jnp.float32)
    ordered = jnp.dot(select, seq_logps, precision=lax.Precision.HIGHEST).reshape(seq_total // 2, 2)
    pair_loss = jax.nn.softplus(-pref_beta * (ordered[:, 0] - ordered[:, 1] - ref_margin))
    live_count = jnp.sum(live_mask.astype(jnp.float32))
    z_loss = zloss_weight * jnp.sum(jnp.where(live_mask, log_norm * log_norm, 0.0)) / live_count
    return (seq_logps, pair_loss, z_loss)


def solution(mesh):
    placed = (P("seq", None), P(None, ("seq", "vocab")), P("seq"), P(), P(), P())
    return jax.shard_map(
        per_device, mesh=mesh, in_specs=placed, out_specs=(P(), P(), P()), check_vma=False
    )
```

profile of v0, /device:TPU:0, one launch (start us, length us, event | category | flops | bytes accessed | tf_op | source)
XLA Modules:
  0.0 195.6 jit_solution(578517166683249568)
XLA Ops:
  7.2 0.0 all-gather.2.cloned.1.call-start
  7.2 0.7 all-gather.2.cloned.1.call-update
  7.9 0.7 iota_compare_fusion
  8.6 0.1 lt.20
  8.7 0.7 eq.32
  9.5 1.2 dynamic-slice
  11.4 0.9 dynamic-update-slice
  12.2 9.5 %all-reduce = s32[960]{0:T(1024)S(1)} all-reduce(s32[960]{0:T(1024)S(1)} %dynamic-update-slice), channel_id=1, replica_groups=mesh['seq'=8,'vocab'=4] {'seq'}, use_global_device_ids=true, to_apply=%add | all-reduce | flops 960 | bytes 7680
  21.7 42.9 %all-gather.2.cloned.1.call-done = bf16[960,4096]{1,0:T(8,128)(2,1)} async-done(((bf16[120,4096]{1,0:T(8,128)(2,1)}), bf16[960,4096]{1,0:T(8,128)(2,1)}) %all-gather.2.cloned.1.call-update) | async-done | bytes 7864336 | tf_op jit(solution)/shard_map/all_gather | solution.py:19
  64.7 32.4 %fusion.7 = (f32[960]{0:T(1024)S(1)}, f32[960,3072]{1,0:T(8,128)}) fusion(bf16[960,4096]{1,0:T(8,128)(2,1)} %all-gather.2.cloned.1.call-done, bf16[4096,3072]{1,0:T(8,128)(2,1)} %param.7), kind=kOutput, calls=%fused_computation.18 | convolution fusion | flops 24162140160 | bytes 44830464 | tf_op jit(solution)/shard_map/dot_general | solution.py:18
  97.1 0.0 copy-start.1
  97.1 0.0 copy-start
  97.1 39.3 %pmax.7 = f32[960]{0:T(1024)S(1)} all-reduce(f32[960]{0:T(1024)S(1)} %get-tuple-element.11), channel_id=1, replica_groups=mesh['seq'=8,'vocab'=4] {'seq','vocab'}, use_global_device_ids=true, to_apply=%region_3.4 | all-reduce | flops 960 | bytes 7680 | tf_op jit(solution)/shard_map/pmax | solution.py:35
  136.4 6.4 %exponential_reduce_fusion = (f32[960]{0:T(1024)S(1)}, f32[960]{0:T(1024)S(1)}) fusion(f32[960,3072]{1,0:T(8,128)} %get-tuple-element.12, f32[960]{0:T(1024)S(1)} %get-tuple-element.11, s32[3072]{0:T(1024)S(1)} %iota_add_fusion, s32[960]{0:T(1024)S(1)} %all-reduce), kind=kLoop, calls=%fused_computation | loop fusion | flops 14743680 | bytes 11824128 | tf_op jit(solution)/shard_map/reduce_sum | solution.py:24
  142.8 41.1 %all-reduce.1 = (f32[960]{0:T(1024)S(1)}, f32[960]{0:T(1024)S(1)}) all-reduce(f32[960]{0:T(1024)S(1)} %get-tuple-element.4, f32[960]{0:T(1024)S(1)} %exponential_multiply_fusion), channel_id=1, replica_groups=mesh['seq'=8,'vocab'=4] {'seq','vocab'}, use_global_device_ids=true, to_apply=%region_1.0 | all-reduce | flops 1920 | bytes 15360 | tf_op jit(solution)/shard_map/psum | solution.py:36
  183.8 0.6 select_reduce_fusion.1
  184.5 0.1 sub.30
  184.5 0.0 copy-done.1
  184.5 0.7 convert_reduce_fusion
  185.3 0.0 copy-start.2
  185.3 0.3 fusion
  185.6 0.1 copy.9
  185.7 0.0 copy-done
  185.7 0.5 compare_select_fusion
  187.6 0.0 copy-done.2
  (3 shorter events, 0.0 us)
Async XLA Ops:
  7.2 57.5 %all-gather.2.cloned.1.call-start = ((), (), s32[]{:S(2)}) async-start(), calls=%async_computation | async-start | bytes 8847360 | tf_op jit(solution)/shard_map/all_gather | solution.py:19
  97.1 87.4 %copy-start.1 = (s32[8]{0:T(128)S(1)}, s32[8]{0:T(128)}, u32[]{:S(2)}) copy-start(s32[8]{0:T(128)} %param.9) | copy-start | bytes 100
  97.1 88.6 %copy-start = (f32[4]{0:T(128)S(1)}, f32[4]{0:T(128)}, u32[]{:S(2)}) copy-start(f32[4]{0:T(128)} %param.11) | copy-start | bytes 52
  185.3 2.3 %copy-start.2 = (f32[8]{0:T(128)}, f32[8]{0:T(128)S(1)}, u32[]{:S(2)}) copy-start(f32[8]{0:T(128)S(1)} %get-tuple-element.6) | copy-start | bytes 100
Sparse Core Ops, SparseCore 0:
  9.9 54.7 all-gather.1
where the time goes:
time: 196 us
  blocking collectives  89.8 us (46%)
  waiting for transfers between devices  43.6 us (22%)
  matrix products  32.7 us (17%)
  between operations  17.2 us (9%)
  other arithmetic  9.04 us (5%)
  local copies, waits for them, and re-layouts  3.11 us (2%)
    all_gather x1, waiting for transfers between devices, per_device(): lax.all_gather(hidden, 'seq', axis=0, tiled=True)  42.9 us
    psum x1, blocking collectives, per_device(): lax.psum((local_sum * jnp.exp(local_max - top_score), picked), ('seq', 'v...  41.1 us
    pmax x1, blocking collectives, per_device(): top_score = lax.pmax(local_max, ('seq', 'vocab'))  39.3 us
    dot_general x1, matrix products, per_device(): jnp.dot(lax.all_gather(hidden, 'seq', axis=0, tiled=True), head_weight, p...  32.4 us
    unnamed x1, blocking collectives  9.49 us
    reduce_sum x1, other arithmetic, per_device(): local_sum = jnp.sum(jnp.exp(logits - local_max[:, None]), axis=1)  6.39 us
  transfers between devices with their start and end apart: 1, of which 1 were waited for; matrix products, arithmetic and copies ran while one was open for 2% of the time, Pallas kernels for 0%

commit v1 on v0

--- a/solution.py
+++ b/solution.py
@@ -34,7 +34,7 @@
     local_max, local_sum, picked = tuple((fresh_part for fresh_part in fresh))
     top_score = lax.pmax(local_max, ("seq", "vocab"))
     exp_total, label_logit = lax.psum(
-        (local_sum * jnp.exp(local_max - top_score), picked), ("seq", "vocab")
+        lax.psum((local_sum * jnp.exp(local_max - top_score), picked), "vocab"), "seq"
     )
     log_norm = (top_score + jnp.log(exp_total)).reshape(seq_total, shard_rows)
     label_logit = label_logit.reshape(seq_total, shard_rows)

time: 196 us -> 178 us (0.908)
  blocking collectives: 89.8 us -> 71.7 us
    psum x1 -> x2, blocking collectives: 41.1 us -> 23 us  [the longest x1 12.2 us: per_device(): lax.psum(lax.psum((local_sum * jnp.exp(local_max - top_score), picked), '...]
where the time goes in v1:
time: 178 us; the launch traced here: 177 us
  blocking collectives  71.7 us (40%)
  waiting for transfers between devices  43.6 us (24%)
  matrix products  32.7 us (18%)
  between operations  17.3 us (10%)
  other arithmetic  9.04 us (5%)
  local copies, waits for them, and re-layouts  3.11 us (2%)
    all_gather x1, waiting for transfers between devices, per_device(): lax.all_gather(hidden, 'seq', axis=0, tiled=True)  42.9 us
    pmax x1, blocking collectives, per_device(): top_score = lax.pmax(local_max, ('seq', 'vocab'))  39.2 us
    dot_general x1, matrix products, per_device(): jnp.dot(lax.all_gather(hidden, 'seq', axis=0, tiled=True), head_weight, p...  32.4 us
    psum x1, blocking collectives, per_device(): lax.psum(lax.psum((local_sum * jnp.exp(local_max - top_score), picked), '...  12.2 us
    psum x1, blocking collectives, per_device(): lax.psum((local_sum * jnp.exp(local_max - top_score), picked), 'vocab')  10.8 us
    unnamed x1, blocking collectives  9.49 us
    reduce_sum x1, other arithmetic, per_device(): local_sum = jnp.sum(jnp.exp(logits - local_max[:, None]), axis=1)  6.39 us
  transfers between devices with their start and end apart: 1, of which 1 were waited for; matrix products, arithmetic and copies ran while one was open for 2% of the time, Pallas kernels for 0%

profile of v1, /device:TPU:0, one launch (start us, length us, event | category | flops | bytes accessed | tf_op | source)
XLA Modules:
  0.0 177.5 jit_solution(12035920809394591059)
XLA Ops:
  7.2 0.0 all-gather.2.cloned.1.call-start
  7.2 0.7 all-gather.2.cloned.1.call-update
  7.9 0.7 iota_compare_fusion
  8.6 0.1 lt.20
  8.7 0.7 eq.32
  9.5 1.2 dynamic-slice
  11.4 0.9 dynamic-update-slice
  12.2 9.5 %all-reduce = s32[960]{0:T(1024)S(1)} all-reduce(s32[960]{0:T(1024)S(1)} %dynamic-update-slice), channel_id=1, replica_groups=mesh['seq'=8,'vocab'=4] {'seq'}, use_global_device_ids=true, to_apply=%add | all-reduce | flops 960 | bytes 7680
  21.7 42.9 %all-gather.2.cloned.1.call-done = bf16[960,4096]{1,0:T(8,128)(2,1)} async-done(((bf16[120,4096]{1,0:T(8,128)(2,1)}), bf16[960,4096]{1,0:T(8,128)(2,1)}) %all-gather.2.cloned.1.call-update) | async-done | bytes 7864336 | tf_op jit(solution)/shard_map/all_gather | solution.py:19
  64.7 32.4 %fusion.7 = (f32[960]{0:T(1024)S(1)}, f32[960,3072]{1,0:T(8,128)}) fusion(bf16[960,4096]{1,0:T(8,128)(2,1)} %all-gather.2.cloned.1.call-done, bf16[4096,3072]{1,0:T(8,128)(2,1)} %param.7), kind=kOutput, calls=%fused_computation.18 | convolution fusion | flops 24162140160 | bytes 44830464 | tf_op jit(solution)/shard_map/dot_general | solution.py:18
  97.1 0.0 copy-start.1
  97.1 0.0 copy-start
  97.1 39.2 %pmax.7 = f32[960]{0:T(1024)S(1)} all-reduce(f32[960]{0:T(1024)S(1)} %get-tuple-element.13), channel_id=1, replica_groups=mesh['seq'=8,'vocab'=4] {'seq','vocab'}, use_global_device_ids=true, to_apply=%region_4.5 | all-reduce | flops 960 | bytes 7680 | tf_op jit(solution)/shard_map/pmax | solution.py:35
  136.3 6.4 %exponential_reduce_fusion = (f32[960]{0:T(1024)S(1)}, f32[960]{0:T(1024)S(1)}) fusion(f32[960,3072]{1,0:T(8,128)} %get-tuple-element.14, f32[960]{0:T(1024)S(1)} %get-tuple-element.13, s32[3072]{0:T(1024)S(1)} %iota_add_fusion, s32[960]{0:T(1024)S(1)} %all-reduce), kind=kLoop, calls=%fused_computation | loop fusion | flops 14743680 | bytes 11824128 | tf_op jit(solution)/shard_map/reduce_sum | solution.py:24
  142.8 10.8 %all-reduce.2 = (f32[960]{0:T(1024)S(1)}, f32[960]{0:T(1024)S(1)}) all-reduce(f32[960]{0:T(1024)S(1)} %get-tuple-element.4, f32[960]{0:T(1024)S(1)} %exponential_multiply_fusion), channel_id=1, replica_groups=mesh['seq'=8,'vocab'=4] {'vocab'}, use_global_device_ids=true, to_apply=%region_1.0 | all-reduce | flops 1920 | bytes 15360 | tf_op jit(solution)/shard_map/psum | solution.py:37
  153.5 12.2 %all-reduce.1 = (f32[960]{0:T(1024)S(1)}, f32[960]{0:T(1024)S(1)}) all-reduce(f32[960]{0:T(1024)S(1)} %get-tuple-element.9, f32[960]{0:T(1024)S(1)} %get-tuple-element.10), channel_id=1, replica_groups=mesh['seq'=8,'vocab'=4] {'seq'}, use_global_device_ids=true, to_apply=%region_2.3 | all-reduce | flops 1920 | bytes 15360 | tf_op jit(solution)/shard_map/psum | solution.py:36
  165.7 0.6 select_reduce_fusion.1
  166.3 0.1 sub.30
  166.4 0.0 copy-done.1
  166.4 0.7 convert_reduce_fusion
  167.2 0.0 copy-start.2
  167.2 0.3 fusion
  167.5 0.1 copy.9
  167.6 0.0 copy-done
  167.6 0.5 compare_select_fusion
  169.5 0.0 copy-done.2
  (3 shorter events, 0.0 us)
Async XLA Ops:
  7.2 57.5 %all-gather.2.cloned.1.call-start = ((), (), s32[]{:S(2)}) async-start(), calls=%async_computation | async-start | bytes 8847360 | tf_op jit(solution)/shard_map/all_gather | solution.py:19
  97.1 69.3 %copy-start.1 = (s32[8]{0:T(128)S(1)}, s32[8]{0:T(128)}, u32[]{:S(2)}) copy-start(s32[8]{0:T(128)} %param.9) | copy-start | bytes 100
  97.1 70.5 %copy-start = (f32[4]{0:T(128)S(1)}, f32[4]{0:T(128)}, u32[]{:S(2)}) copy-start(f32[4]{0:T(128)} %param.11) | copy-start | bytes 52
  167.2 2.3 %copy-start.2 = (f32[8]{0:T(128)}, f32[8]{0:T(128)S(1)}, u32[]{:S(2)}) copy-start(f32[8]{0:T(128)S(1)} %get-tuple-element.6) | copy-start | bytes 100
Sparse Core Ops, SparseCore 0:
  9.9 54.7 all-gather.1
